TPU v7x, 32 devices: a whole 2x2x4 slice. The times are simulated.
32 devices in a mesh: depth: 4 (over z), rows: 8 (over y, x, core).
Axes of the slice: x: 2, y: 2, z: 4, core: 2. Of those that a mesh axis runs over, the one named last changes fastest.
Arguments:
- target: float32 [4, 2, 4096, 4096], P('depth', None, 'rows'), may hold values from -6 to 6
- depth_index: int32 [4], P('depth'), may hold values from 0 to 255
- band_mask: int32 [4, 2, 4096], P('depth'), may hold values from 0 to 1, as said below
Outputs:
- hologram: float32 [2, 4096, 4096], P(None, ('depth', 'rows'))
Inputs may be any that keep to these rules, and one draw needn't show every extreme that they name: `band_mask`: for each plane and each of the two dimensions, the ones are exactly the frequency indices k with min(k, 4096 - k) below a cutoff between 512 and 2048.
All inputs are finite; a program needn't handle non-finite values.
Results may differ from a plain program's by a relative error of at most 0.0009.
Values sent between devices are 32-bit elements; how exact they have to be, the bound alone decides.
A program may use at most 128 MiB of HBM per device.

v0:
```python
import functools
import math

import jax
import jax.numpy as jnp
import numpy as np
from jax import lax
from jax.experimental import pallas as pl
from jax.experimental.pallas import tpu as pltpu
from jax.sharding import PartitionSpec as P


LOW = 32
HIGH = 128
N = LOW * HIGH
VMEM_LIMIT = 56 * 1024 * 1024


def scaled(value, factor_real, factor_imaginary):
    real, imaginary = value
    if abs(factor_imaginary) < 1e-12:
        if factor_real > 0:
            return (real, imaginary)
        return (-real, -imaginary)
    if abs(factor_real) < 1e-12:
        if factor_imaginary > 0:
            return (-imaginary, real)
        return (imaginary, -real)
    a, b = np.float32(factor_real), np.float32(factor_imaginary)
    return (real * a - imaginary * b, real * b + imaginary * a)


def root(numerator, length, direction):
    angle = direction * 2.0 * math.pi * (numerator % length) / length
    return math.cos(angle), math.sin(angle)


def add(left, right):
    return (left[0] + right[0], left[1] + right[1])


def subtract(left, right):
    return (left[0] - right[0], left[1] - right[1])


def butterfly(values, direction):
    count = len(values)
    if count == 1:
        return values
    even = butterfly(values[0::2], direction)
    odd = butterfly(values[1::2], direction)
    odd = [scaled(v, *root(k, count, direction)) for k, v in enumerate(odd)]
    return [add(e, o) for e, o in zip(even, odd)] + [subtract(e, o) for e, o in zip(even, odd)]


def dense_table(direction):
    index = np.arange(HIGH)
    angles = direction * 2.0 * np.pi / HIGH * (index[:, None] * index[None, :] % HIGH)
    cosine, sine = np.cos(angles), np.sin(angles)
    return np.block([[cosine, -sine], [sine, cosine]])


def halves(table):
    high = table.astype(np.float32).astype(jnp.bfloat16)
    low = (table - high.astype(np.float64)).astype(np.float32).astype(jnp.bfloat16)
    return jnp.asarray(high), jnp.asarray(low)


def twiddles(direction, scaling):
    product = np.arange(LOW)[:, None] * np.arange(HIGH)[None, :] % N
    angles = direction * 2.0 * np.pi / N * product
    return (
        jnp.asarray((np.cos(angles) * scaling).astype(np.float32)),
        jnp.asarray((np.sin(angles) * scaling).astype(np.float32)),
    )


def split(value):
    high = value.astype(jnp.bfloat16)
    return high, (value - high.astype(jnp.float32)).astype(jnp.bfloat16)


def tripled(value):
    high, low = split(value)
    return jnp.concatenate([high, low, high], axis=0)


def dot(left, right):
    return jnp.dot(left, right, preferred_element_type=jnp.float32)


def width_kernel(chunk, chunks, owners, x_ref, tr_ref, ti_ref, th_ref, tl_ref, o_ref, hi_ref, lo_ref):
    tile = x_ref.shape[1]

    def body(step, carry):
        rows = pl.ds(pl.multiple_of(step * 16, 16), 16)
        values = []
        for first in range(owners):
            total = None
            for second in range(chunks):
                at = (first + owners * second) * HIGH
                value = (x_ref[0, rows, at:at + HIGH], x_ref[1, rows, at:at + HIGH])
                value = scaled(value, *root(chunk * second, chunks, -1.0))
                total = value if total is None else add(total, value)
            values.append(scaled(total, *root(chunk * first, LOW, -1.0)))
        for owner, (real, imaginary) in enumerate(butterfly(values, -1.0)):
            k = chunks * owner + chunk
            turn_real, turn_imaginary = tr_ref[k:k + 1, :], ti_ref[k:k + 1, :]
            high, low = split(real * turn_real - imaginary * turn_imaginary)
            hi_ref[owner, rows, :HIGH] = high
            lo_ref[owner, rows, :HIGH] = low
            high, low = split(real * turn_imaginary + imaginary * turn_real)
            hi_ref[owner, rows, HIGH:] = high
            lo_ref[owner, rows, HIGH:] = low
        return carry

    lax.fori_loop(0, tile // 16, body, 0)
    for owner in range(owners):
        high = hi_ref[owner]
        out = dot(high, th_ref[...]) + dot(lo_ref[owner], th_ref[...]) + dot(high, tl_ref[...])
        o_ref[owner, 0] = out[:, :HIGH]
        o_ref[owner, 1] = out[:, HIGH:]


def along_width(field, chunk, chunks, owners, tables):
    _, height, _ = field.shape
    tile = min(128, height)
    whole = lambda a: pl.BlockSpec(a.shape, lambda i: (0,) * a.ndim)
    return pl.pallas_call(
        functools.partial(width_kernel, chunk, chunks, owners),
        grid=(height // tile,),
        in_specs=[pl.BlockSpec((2, tile, N), lambda i: (0, i, 0))] + [whole(a) for a in tables],
        out_specs=pl.BlockSpec((owners, 2, tile, HIGH), lambda i: (0, 0, i, 0)),
        out_shape=jax.ShapeDtypeStruct((owners, 2, height, HIGH), jnp.float32),
        scratch_shapes=[pltpu.VMEM((owners, tile, 2 * HIGH), jnp.bfloat16)] * 2,
        compiler_params=pltpu.CompilerParams(vmem_limit_bytes=VMEM_LIMIT),
        cost_estimate=pl.CostEstimate(flops=6 * height * HIGH * HIGH * 4 * owners * 2, bytes_accessed=field.size * 4 + field.size * 4 // chunks, transcendentals=0),
    )(field, *tables)


def series(values, points):
    nodes = np.cos(np.pi * (np.arange(400) + 0.5) / 400) * 0.125 + 0.125
    basis = np.polynomial.chebyshev.Chebyshev.fit(nodes, values(np.sqrt(nodes)), points, domain=[0.0, 0.25])
    return [np.float32(c) for c in basis.convert(kind=np.polynomial.Polynomial).coef]


COSINE = series(lambda r: np.cos(2.0 * np.pi * r), 6)
SINE = series(lambda r: np.sin(2.0 * np.pi * r) / r, 6)


def horner(coefficients, at):
    total = coefficients[-1]
    for c in coefficients[-2::-1]:
        total = total * at + c
    return total


def signed(natural):
    return jnp.where(natural < N // 2, natural, natural - N).astype(jnp.float32)


def column_kernel(scalars_ref, x_ref, tr_ref, ti_ref, f_ref, i_ref, o_ref, work_ref):
    owners, _, pieces, _, _ = x_ref.shape
    distance = scalars_ref[0].astype(jnp.float32) * 2.0 + 100.0
    limit_height = scalars_ref[1].astype(jnp.float32)
    limit_width = scalars_ref[2].astype(jnp.float32)
    column = scalars_ref[3]

    def forward(step, carry):
        rows = pl.ds(pl.multiple_of(step * 8, 8), 8)
        low_rows = pl.ds(pl.multiple_of(step * 8 + HIGH, 8), 8)
        values = [(x_ref[s, 0, p, rows, :], x_ref[s, 1, p, rows, :]) for s in range(owners) for p in range(pieces)]
        for k, (real, imaginary) in enumerate(butterfly(values, -1.0)):
            work_ref[k, rows, :] = real
            work_ref[k, low_rows, :] = imaginary
        return carry

    lax.fori_loop(0, HIGH // 8, forward, 0)

    across = signed(lax.broadcasted_iota(jnp.int32, (1, HIGH), 1) * LOW + column)
    inside_width = jnp.abs(across) < limit_width
    across_square = (across * (1.0 / N)) ** 2

    def turned(k):
        real, imaginary = work_ref[k, :HIGH, :], work_ref[k, HIGH:, :]
        turn_real, turn_imaginary = tr_ref[k], ti_ref[k]
        return jnp.concatenate(
            [real * turn_real - imaginary * turn_imaginary, real * turn_imaginary + imaginary * turn_real], axis=0
        )

    def propagate(k, real, imaginary):
        down = signed(lax.broadcasted_iota(jnp.int32, (HIGH, HIGH), 0) * LOW + k)
        square = (down * (1.0 / N)) ** 2 + across_square
        rest_square = 4.0 - square
        drop = 2.0 - rest_square * lax.rsqrt(rest_square)
        turns = -distance * (0.25 * (square + drop * drop))
        rest = turns - jnp.floor(turns + 0.5)
        at = rest * rest
        keep = jnp.logical_and(jnp.abs(down) < limit_height, inside_width)
        cosine = jnp.where(keep, horner(COSINE, at), 0.0)
        sine = jnp.where(keep, horner(SINE, at) * rest, 0.0)
        return jnp.concatenate([real * cosine - imaginary * sine, real * sine + imaginary * cosine], axis=0)

    def middle(step, carry):
        pair = [2 * step, 2 * step + 1]
        spectrum = dot(f_ref[...], tripled(jnp.concatenate([turned(k) for k in pair], axis=1)))
        moved = [
            propagate(k, spectrum[:HIGH, i * HIGH:(i + 1) * HIGH], spectrum[HIGH:, i * HIGH:(i + 1) * HIGH])
            for i, k in enumerate(pair)
        ]
        back = dot(i_ref[...], tripled(jnp.concatenate(moved, axis=1)))
        for i, k in enumerate(pair):
            real, imaginary = back[:HIGH, i * HIGH:(i + 1) * HIGH], back[HIGH:, i * HIGH:(i + 1) * HIGH]
            turn_real, turn_imaginary = tr_ref[k], ti_ref[k]
            work_ref[k, :HIGH, :] = real * turn_real + imaginary * turn_imaginary
            work_ref[k, HIGH:, :] = imaginary * turn_real - real * turn_imaginary
        return carry

    lax.fori_loop(0, LOW // 2, middle, 0)

    def inverse(step, carry):
        rows = pl.ds(pl.multiple_of(step * 8, 8), 8)
        low_rows = pl.ds(pl.multiple_of(step * 8 + HIGH, 8), 8)
        values = [(work_ref[k, rows, :], work_ref[k, low_rows, :]) for k in range(LOW)]
        for j, (real, imaginary) in enumerate(butterfly(values, 1.0)):
            o_ref[j, 0, rows, :] = real
            o_ref[j, 1, rows, :] = imaginary
        return carry

    lax.fori_loop(0, HIGH // 8, inverse, 0)


def columns_step(received, scalars, tables):
    owners, _, height, _ = received.shape
    received = received.reshape(owners, 2, height // HIGH, HIGH, HIGH)
    vmem = pl.BlockSpec(memory_space=pltpu.VMEM)
    return pl.pallas_call(
        column_kernel,
        in_specs=[pl.BlockSpec(memory_space=pltpu.SMEM)] + [vmem] * (1 + len(tables)),
        out_specs=vmem,
        out_shape=jax.ShapeDtypeStruct((LOW, 2, HIGH, HIGH), jnp.float32),
        scratch_shapes=[pltpu.VMEM((LOW, 2 * HIGH, HIGH), jnp.float32)],
        compiler_params=pltpu.CompilerParams(vmem_limit_bytes=VMEM_LIMIT),
        cost_estimate=pl.CostEstimate(flops=12 * LOW * HIGH * 256 * 256 * 2, bytes_accessed=16 * 1024 * 1024, transcendentals=0),
    )(scalars, received, *tables)


def output_kernel(chunks, *refs):
    inputs = refs[:chunks]
    tr_ref, ti_ref, th_ref, tl_ref, o_ref, work_ref = refs[chunks:]
    owners, _, height, _ = inputs[0].shape
    for owner in range(owners):
        for chunk in range(chunks):
            k = chunks * owner + chunk
            value = jnp.concatenate([inputs[chunk][owner, 0], inputs[chunk][owner, 1]], axis=1)
            high, low = split(value)
            out = dot(high, th_ref[...]) + dot(low, th_ref[...]) + dot(high, tl_ref[...])
            real, imaginary = out[:, :HIGH], out[:, HIGH:]
            turn_real, turn_imaginary = tr_ref[k:k + 1, :], ti_ref[k:k + 1, :]
            work_ref[k, 0] = real * turn_real - imaginary * turn_imaginary
            work_ref[k, 1] = real * turn_imaginary + imaginary * turn_real

    def body(step, carry):
        rows = pl.ds(pl.multiple_of(step * 8, 8), 8)
        values = [(work_ref[k, 0, rows, :], work_ref[k, 1, rows, :]) for k in range(LOW)]
        for j, (real, imaginary) in enumerate(butterfly(values, 1.0)):
            o_ref[0, rows, j * HIGH:(j + 1) * HIGH] = real
            o_ref[1, rows, j * HIGH:(j + 1) * HIGH] = imaginary
        return carry

    lax.fori_loop(0, height // 8, body, 0)


def inverse_width(parts, tables):
    height = parts[0].shape[2]
    vmem = pl.BlockSpec(memory_space=pltpu.VMEM)
    return pl.pallas_call(
        functools.partial(output_kernel, len(parts)),
        in_specs=[vmem] * (len(parts) + len(tables)),
        out_specs=vmem,
        out_shape=jax.ShapeDtypeStruct((2, height, N), jnp.float32),
        scratch_shapes=[pltpu.VMEM((LOW, 2, height, HIGH), jnp.float32)],
        compiler_params=pltpu.CompilerParams(vmem_limit_bytes=VMEM_LIMIT),
        cost_estimate=pl.CostEstimate(flops=6 * LOW * height * 256 * 256, bytes_accessed=8 * height * N * 2, transcendentals=0),
        name="output",
    )(*parts, *tables)


def local(target, depth_index, band_mask):
    owners, depths = lax.axis_size("rows"), lax.axis_size("depth")
    chunks = LOW // owners
    field = target.reshape(target.shape[1:])
    scale = 1.0 / math.sqrt(N)
    forward, backward = dense_table(-1.0), dense_table(1.0)
    left = tuple(jnp.concatenate([h, h, l], axis=1) for h, l in (halves(forward), halves(backward)))
    forward_right, backward_right = halves(forward.T), halves(backward.T)
    turn = twiddles(-1.0, scale)
    turn_back = twiddles(1.0, scale / math.sqrt(depths))
    spread = tuple(jnp.broadcast_to(t[:, :, None], (LOW, HIGH, HIGH)) for t in turn)
    limits = (jnp.sum(band_mask[0], axis=-1) + 1) // 2
    me = lax.axis_index("rows")
    rows = N // (owners * depths)

    pieces = []
    for chunk in range(chunks):
        sent = along_width(field, chunk, chunks, owners, turn + forward_right)
        received = lax.all_to_all(sent, "rows", split_axis=0, concat_axis=0, tiled=True)
        scalars = jnp.stack([depth_index[0], limits[0], limits[1], me * chunks + chunk]).astype(jnp.int32)
        part = columns_step(received, scalars, spread + left)
        pieces.append(lax.psum_scatter(part, "depth", scatter_dimension=0, tiled=True))
    results = []
    for share in pieces:
        share = share.reshape(share.shape[0], 2, HIGH // rows, rows, HIGH)
        share = jnp.transpose(share, (0, 2, 1, 3, 4)).reshape(owners, 2, rows, HIGH)
        results.append(lax.all_to_all(share, "rows", split_axis=0, concat_axis=0, tiled=True))
    return inverse_width(results, turn_back + backward_right)


MESH = pl.DeviceIdType.MESH
PART = 32
PARTS = HIGH // PART
AHEAD = 3


def slots():
    half = PART // 2
    order = []
    for part in range(PARTS):
        order += list(range(half * part, half * (part + 1)))
        order += list(range(HIGH - half * (part + 1), HIGH - half * part))
    return np.array(order)


def both(index):
    return np.concatenate([index, index + HIGH])


def nt_dot(left, right):
    return lax.dot_general(left, right, (((1,), (1,)), ((), ())), preferred_element_type=jnp.float32)


def spread_kernel(chunks, x_ref, tr_ref, ti_ref, th_ref, tl_ref, o_ref, work_ref):
    def body(step, carry):
        rows = pl.ds(pl.multiple_of(step * 8, 8), 8)
        values = [(x_ref[0, rows, g * HIGH:(g + 1) * HIGH], x_ref[1, rows, g * HIGH:(g + 1) * HIGH]) for g in range(LOW)]
        for k, (real, imaginary) in enumerate(butterfly(values, -1.0)):
            turn_real, turn_imaginary = tr_ref[k:k + 1, :], ti_ref[k:k + 1, :]
            work_ref[k, rows, :HIGH] = real * turn_real - imaginary * turn_imaginary
            work_ref[k, rows, HIGH:] = real * turn_imaginary + imaginary * turn_real
        return carry

    lax.fori_loop(0, HIGH // 8, body, 0)

    def dense(step, carry):
        value = jnp.concatenate([work_ref[2 * step], work_ref[2 * step + 1]], axis=0)
        high, low = split(value)
        out = nt_dot(th_ref[...], high) + nt_dot(th_ref[...], low) + nt_dot(tl_ref[...], high)
        for i in range(2):
            k = 2 * step + i
            owner, chunk = k // chunks, k % chunks
            for part in range(PARTS):
                for side in range(2):
                    at = side * HIGH + part * PART
                    o_ref[chunk * PARTS + part, owner, 0, side] = out[at:at + PART, i * HIGH:(i + 1) * HIGH]
        return carry

    lax.fori_loop(0, LOW // 2, dense, 0)


def spread_width(field, chunks, owners, tables):
    _, height, _ = field.shape
    whole = lambda a: pl.BlockSpec(a.shape, lambda i: (0,) * a.ndim)
    shape = (chunks * PARTS, owners, height // HIGH, 2, PART, HIGH)
    return pl.pallas_call(
        functools.partial(spread_kernel, chunks),
        grid=(height // HIGH,),
        in_specs=[pl.BlockSpec((2, HIGH, N), lambda i: (0, i, 0))] + [whole(a) for a in tables],
        out_specs=pl.BlockSpec(shape[:2] + (1,) + shape[3:], lambda i: (0, 0, i, 0, 0, 0)),
        out_shape=jax.ShapeDtypeStruct(shape, jnp.float32),
        scratch_shapes=[pltpu.VMEM((LOW, HIGH, 2 * HIGH), jnp.float32)],
        compiler_params=pltpu.CompilerParams(vmem_limit_bytes=VMEM_LIMIT),
        name="spread",
    )(field, *tables)


def line_kernel(chunks, owners, depths, scalars_ref, tr_ref, ti_ref, fh_ref, fl_ref, ih_ref, il_ref, sent_ref, back_ref,
                buf, rbuf, lbuf, work_ref, self_f, send_f, recv_f, send_r, recv_r, send_l, recv_l, self_b, send_b, recv_b):
    total = chunks * PARTS
    block = LOW // depths
    pieces = LOW // owners
    here, me = lax.axis_index("depth"), lax.axis_index("rows")
    last = depths - 1 - here

    barrier = pltpu.get_barrier_semaphore()
    for step in range(1, owners):
        pl.semaphore_signal(barrier, inc=1, device_id=(here, (me + step) % owners), device_id_type=MESH)

    @pl.when(here > 0)
    def _():
        pl.semaphore_signal(barrier, inc=1, device_id=(here - 1, me), device_id_type=MESH)

    @pl.when(last > 0)
    def _():
        pl.semaphore_signal(barrier, inc=1, device_id=(here + 1, me), device_id_type=MESH)

    pl.semaphore_wait(barrier, owners - 1 + jnp.minimum(here, 1) + jnp.minimum(last, 1))

    def own_copy(t):
        return pltpu.make_async_copy(sent_ref.at[t, me], buf.at[t, pl.ds(me * pieces, pieces)], self_f.at[t])

    def start_forward(t):
        own_copy(t).start()
        for step in range(1, owners):
            peer = (me + step) % owners
            pltpu.make_async_remote_copy(
                src_ref=sent_ref.at[t, peer],
                dst_ref=buf.at[t, pl.ds(me * pieces, pieces)],
                send_sem=send_f.at[t],
                recv_sem=recv_f.at[t],
                device_id=(here, peer),
                device_id_type=MESH,
            ).start()

    def others(t, sem):
        some = buf.at[t, pl.ds(0, pieces * (owners - 1))]
        return pltpu.make_async_copy(some, some, sem.at[t])

    def right_copy(t, q):
        return pltpu.make_async_remote_copy(
            src_ref=buf.at[t, pl.ds(q * block, block)],
            dst_ref=rbuf.at[t, q - 1],
            send_sem=send_r.at[t, q - 1],
            recv_sem=recv_r.at[t, q - 1],
            device_id=(here + 1, me),
            device_id_type=MESH,
        )

    def left_copy(t, q):
        return pltpu.make_async_remote_copy(
            src_ref=buf.at[t, pl.ds(q * block, block)],
            dst_ref=lbuf.at[t, q],
            send_sem=send_l.at[t, q],
            recv_sem=recv_l.at[t, q],
            device_id=(here - 1, me),
            device_id_type=MESH,
        )

    def final_copy(t, peer):
        return pltpu.make_async_remote_copy(
            src_ref=buf.at[t, here * block + peer],
            dst_ref=back_ref.at[t, me],
            send_sem=send_b.at[t],
            recv_sem=recv_b.at[t],
            device_id=(here, peer),
            device_id_type=MESH,
        )

    def final_own(t):
        return pltpu.make_async_copy(buf.at[t, here * block + me], back_ref.at[t, me], self_b.at[t])

    def finals(t, sem):
        some = back_ref.at[t, pl.ds(0, owners - 1)]
        return pltpu.make_async_copy(some, some, sem.at[t])

    distance = scalars_ref[0].astype(jnp.float32) * 2.0 + 100.0
    limit_height = scalars_ref[1].astype(jnp.float32)
    limit_width = scalars_ref[2].astype(jnp.float32)

    def columns(t):
        def forward(step, carry):
            rows = pl.ds(pl.multiple_of(step * 8, 8), 8)
            values = [(buf[t, p, 0, rows, :], buf[t, p, 1, rows, :]) for p in range(LOW)]
            for k, (real, imaginary) in enumerate(butterfly(values, -1.0)):
                work_ref[k, 0, rows, :] = real
                work_ref[k, 1, rows, :] = imaginary
            return carry

        lax.fori_loop(0, PART // 8, forward, 0)

        column = me * chunks + t // PARTS
        part = t % PARTS
        half = PART // 2
        slot = lax.broadcasted_iota(jnp.int32, (PART, HIGH), 0)
        turn = jnp.where(slot < half, half * part + slot, slot - half - half * (part + 1))
        across = (column + LOW * turn).astype(jnp.float32)
        inside_width = jnp.abs(across) < limit_width
        across_square = (across * (1.0 / N)) ** 2
        lanes = lax.broadcasted_iota(jnp.int32, (1, HIGH), 1) * LOW
        group = 8

        def middle(step, carry):
            taken = []
            for i in range(group):
                k = group * step + i
                real, imaginary = work_ref[k, 0], work_ref[k, 1]
                turn_real, turn_imaginary = tr_ref[pl.ds(k, 1), :], ti_ref[pl.ds(k, 1), :]
                taken.append(jnp.concatenate(
                    [real * turn_real - imaginary * turn_imaginary, real * turn_imaginary + imaginary * turn_real], axis=1))
            high, low = split(jnp.concatenate(taken, axis=0))
            spectrum = dot(high, fh_ref[...]) + dot(low, fh_ref[...]) + dot(high, fl_ref[...])
            moved = []
            for i in range(group):
                real, imaginary = spectrum[i * PART:(i + 1) * PART, :HIGH], spectrum[i * PART:(i + 1) * PART, HIGH:]
                down = signed(lanes + (group * step + i))
                square = (down * (1.0 / N)) ** 2 + across_square
                rest_square = 4.0 - square
                drop = 2.0 - rest_square * lax.rsqrt(rest_square)
                turns = -distance * (0.25 * (square + drop * drop))
                rest = turns - jnp.floor(turns + 0.5)
                at = rest * rest
                keep = jnp.logical_and(jnp.abs(down) < limit_height, inside_width)
                cosine = jnp.where(keep, horner(COSINE, at), 0.0)
                sine = jnp.where(keep, horner(SINE, at) * rest, 0.0)
                moved.append(jnp.concatenate([real * cosine - imaginary * sine, real * sine + imaginary * cosine], axis=1))
            high, low = split(jnp.concatenate(moved, axis=0))
            back = dot(high, ih_ref[...]) + dot(low, ih_ref[...]) + dot(high, il_ref[...])
            for i in range(group):
                k = group * step + i
                real, imaginary = back[i * PART:(i + 1) * PART, :HIGH], back[i * PART:(i + 1) * PART, HIGH:]
                turn_real, turn_imaginary = tr_ref[pl.ds(k, 1), :], ti_ref[pl.ds(k, 1), :]
                work_ref[k, 0] = real * turn_real + imaginary * turn_imaginary
                work_ref[k, 1] = imaginary * turn_real - real * turn_imaginary
            return carry

        lax.fori_loop(0, LOW // group, middle, 0)

        def inverse(step, carry):
            rows = pl.ds(pl.multiple_of(step * 8, 8), 8)
            values = [(work_ref[k, 0, rows, :], work_ref[k, 1, rows, :]) for k in range(LOW)]
            for j, (real, imaginary) in enumerate(butterfly(values, 1.0)):
                buf[t, j, 0, rows, :] = real
                buf[t, j, 1, rows, :] = imaginary
            return carry

        lax.fori_loop(0, PART // 8, inverse, 0)

    def merge(t, q, other, at):
        def body(j, carry):
            buf[t, q * block + j] += other[t, at, j]
            return carry

        lax.fori_loop(0, block, body, 0)

    for t in range(min(AHEAD, total)):
        start_forward(t)

    def step(t, carry):
        @pl.when(t + AHEAD < total)
        def _():
            start_forward(t + AHEAD)

        @pl.when(t < total)
        def _():
            own_copy(t).wait()
            others(t, recv_f).wait()
            columns(t)

        right = t - here

        @pl.when(jnp.logical_and(right >= 0, right < total))
        def _():
            for q in range(depths - 1, 0, -1):
                @pl.when(jnp.logical_and(here > 0, q >= here))
                def _():
                    right_copy(right, q).wait_recv()
                    merge(right, q, rbuf, q - 1)

                @pl.when(q > here)
                def _():
                    right_copy(right, q).start()

        left = t - last

        @pl.when(jnp.logical_and(left >= 0, left < total))
        def _():
            for q in range(depths - 1):
                @pl.when(jnp.logical_and(last > 0, q <= here))
                def _():
                    left_copy(left, q).wait_recv()
                    merge(left, q, lbuf, q)

                @pl.when(q < here)
                def _():
                    left_copy(left, q).start()

        done = t - jnp.maximum(here, last)

        @pl.when(jnp.logical_and(done >= 0, done < total))
        def _():
            final_own(done).start()
            for step in range(1, owners):
                final_copy(done, (me + step) % owners).start()

        return carry

    lax.fori_loop(0, total + depths - 1, step, 0)

    def finish(t, carry):
        others(t, send_f).wait()
        for q in range(1, depths):
            @pl.when(q > here)
            def _():
                right_copy(t, q).wait_send()
        for q in range(depths - 1):
            @pl.when(q < here)
            def _():
                left_copy(t, q).wait_send()
        final_own(t).wait()
        finals(t, send_b).wait()
        finals(t, recv_b).wait()
        return carry

    lax.fori_loop(0, total, finish, 0)


def line(sent, scalars, tables, chunks, owners, depths):
    total = chunks * PARTS
    block = LOW // depths
    vmem = pl.BlockSpec(memory_space=pltpu.VMEM)
    hbm = pl.BlockSpec(memory_space=pl.ANY)
    dma = pltpu.SemaphoreType.DMA
    tile = (2, PART, HIGH)
    return pl.pallas_call(
        functools.partial(line_kernel, chunks, owners, depths),
        in_specs=[pl.BlockSpec(memory_space=pltpu.SMEM)] + [vmem] * len(tables) + [hbm],
        out_specs=hbm,
        out_shape=jax.ShapeDtypeStruct((total, owners) + tile, jnp.float32),
        scratch_shapes=[
            pltpu.VMEM((total, LOW) + tile, jnp.float32),
            pltpu.VMEM((total, depths - 1, block) + tile, jnp.float32),
            pltpu.VMEM((total, depths - 1, block) + tile, jnp.float32),
            pltpu.VMEM((LOW,) + tile, jnp.float32),
            dma((total,)), dma((total,)), dma((total,)),
            dma((total, depths - 1)), dma((total, depths - 1)),
            dma((total, depths - 1)), dma((total, depths - 1)),
            dma((total,)), dma((total,)), dma((total,)),
        ],
        compiler_params=pltpu.CompilerParams(vmem_limit_bytes=VMEM_LIMIT, collective_id=0, has_side_effects=True),
        name="line",
    )(scalars, *tables, sent)


def gather_kernel(chunks, in_ref, tr_ref, ti_ref, th_ref, tl_ref, o_ref, work_ref):
    def dense(k, carry):
        owner, chunk = k // chunks, k % chunks
        sides = [
            jnp.concatenate([in_ref[chunk * PARTS + part, owner, side] for part in range(PARTS)], axis=0).T for side in range(2)
        ]
        high, low = split(jnp.concatenate(sides, axis=1))
        out = dot(high, th_ref[...]) + dot(low, th_ref[...]) + dot(high, tl_ref[...])
        real, imaginary = out[:, :HIGH], out[:, HIGH:]
        turn_real, turn_imaginary = tr_ref[pl.ds(k, 1), :], ti_ref[pl.ds(k, 1), :]
        work_ref[k, 0] = real * turn_real - imaginary * turn_imaginary
        work_ref[k, 1] = real * turn_imaginary + imaginary * turn_real
        return carry

    lax.fori_loop(0, LOW, dense, 0, unroll=4)

    def body(step, carry):
        rows = pl.ds(pl.multiple_of(step * 8, 8), 8)
        values = [(work_ref[k, 0, rows, :], work_ref[k, 1, rows, :]) for k in range(LOW)]
        for j, (real, imaginary) in enumerate(butterfly(values, 1.0)):
            o_ref[0, rows, j * HIGH:(j + 1) * HIGH] = real
            o_ref[1, rows, j * HIGH:(j + 1) * HIGH] = imaginary
        return carry

    lax.fori_loop(0, HIGH // 8, body, 0)


def gather_width(parts, chunks, tables):
    vmem = pl.BlockSpec(memory_space=pltpu.VMEM)
    return pl.pallas_call(
        functools.partial(gather_kernel, chunks),
        in_specs=[vmem] * (1 + len(tables)),
        out_specs=vmem,
        out_shape=jax.ShapeDtypeStruct((2, HIGH, N), jnp.float32),
        scratch_shapes=[pltpu.VMEM((LOW, 2, HIGH, HIGH), jnp.float32)],
        compiler_params=pltpu.CompilerParams(vmem_limit_bytes=VMEM_LIMIT),
        name="gather",
    )(parts, *tables)


def fused(target, depth_index, band_mask):
    owners, depths = lax.axis_size("rows"), lax.axis_size("depth")
    chunks = LOW // owners
    field = target.reshape(target.shape[1:])
    scale = 1.0 / math.sqrt(N)
    forward, backward = dense_table(-1.0), dense_table(1.0)
    order = both(slots())
    turn = twiddles(-1.0, scale)
    turn_back = twiddles(1.0, scale / math.sqrt(depths))
    limits = (jnp.sum(band_mask[0], axis=-1) + 1) // 2
    scalars = jnp.stack([depth_index[0], limits[0], limits[1]]).astype(jnp.int32)
    sent = spread_width(field, chunks, owners, turn + halves(forward[order]))
    parts = line(sent, scalars, turn + halves(forward.T) + halves(backward.T), chunks, owners, depths)
    return gather_width(parts, chunks, turn_back + halves(backward.T[order]))


def solution(mesh):
    in_specs = (P("depth", None, "rows", None), P("depth"), P("depth", None, None))
    out_specs = P(None, ("depth", "rows"), None)
    step = jax.shard_map(local, mesh=mesh, in_specs=in_specs, out_specs=out_specs, check_vma=False)
    if mesh.shape["rows"] * mesh.shape["depth"] == LOW and mesh.shape["depth"] > 1:
        return jax.shard_map(fused, mesh=mesh, in_specs=in_specs, out_specs=out_specs, check_vma=False)
    return step
```

profile of v0, /device:TPU:0, one launch (start us, length us, event | category | flops | bytes accessed | tf_op | source)
XLA Modules:
  0.0 353.8 jit_solution(18235508013819685189)
XLA Ops:
  0.7 0.9 reduce_sum.9
  1.6 0.6 pad_add_fusion.scalars_ref
  2.2 31.3 %spread.1.sent_ref = f32[16,8,4,2,32,128]{5,4,3,2,1,0:T(8,128)} custom-call(f32[2,512,4096]{2,1,0:T(8,128)} %bitcast.1, f32[32,128]{1,0:T(8,128)} %constant.36.clone.tr_ref, f32[32,128]{1,0:T(8,128)} %constant.37.clone.ti_ref, bf16[256,256]{1,0:T(8,128)(2,1)} %constant.40.clone.th_ref, bf16[256,256]{1,0:T(8,128)(2,1)} %constant.41.clone.tl_ref), custom_call_target="tpu_custom_call" | custom-call | tf_op jit(solution)/shard_map/spread/pallas_call | solution.py:374
  33.4 310.7 %line.1.in_ref = f32[16,8,2,32,128]{4,3,2,1,0:T(8,128)} custom-call(s32[3]{0:T(128)} %pad_add_fusion.scalars_ref, f32[32,128]{1,0:T(8,128)} %constant.36.clone.tr_ref, f32[32,128]{1,0:T(8,128)} %constant.37.clone.ti_ref, bf16[256,256]{1,0:T(8,128)(2,1)} %constant.42.clone.fh_ref, bf16[256,256]{1,0:T(8,128)(2,1)} %constant.43.clone.fl_ref, ...), custom_call_target="tpu_custom_call" | custom-call | tf_op jit(solution)/shard_map/line/pallas_call | solution.py:623
  344.1 9.7 %gather.1 = f32[2,128,4096]{2,1,0:T(8,128)} custom-call(f32[16,8,2,32,128]{4,3,2,1,0:T(8,128)} %line.1.in_ref, f32[32,128]{1,0:T(8,128)} %constant.38.clone.tr_ref, f32[32,128]{1,0:T(8,128)} %constant.39.clone.ti_ref, bf16[256,256]{1,0:T(8,128)(2,1)} %constant.40.clone.th_ref, bf16[256,256]{1,0:T(8,128)(2,1)} %constant.41.clone.tl_ref), custom_call_target="tpu_custom_call" | custom-call | tf_op jit(solution)/shard_map/gather/pallas_call | solution.py:672
  (1 shorter events, 0.0 us)
where the time goes:
time: 354 us
  Pallas kernels  352 us (99%)
    pallas_call x1, Pallas kernels, line(): pl.pallas_call(functools.partial(line_kernel, chunks, owners, depths), in...  311 us
    pallas_call x1, Pallas kernels, spread_width(): pl.pallas_call(functools.partial(spread_kernel, chunks), grid=(height //...  31.3 us
    pallas_call x1, Pallas kernels, gather_width(): pl.pallas_call(functools.partial(gather_kernel, chunks), in_specs=[vmem]...  9.66 us

commit v1 on v0

--- a/solution.py
+++ b/solution.py
@@ -317,9 +317,9 @@
 
 
 MESH = pl.DeviceIdType.MESH
-PART = 32
+PART = 16
 PARTS = HIGH // PART
-AHEAD = 3
+LINE_VMEM = 62 * 1024 * 1024
 
 
 def slots():
@@ -339,57 +339,95 @@
     return lax.dot_general(left, right, (((1,), (1,)), ((), ())), preferred_element_type=jnp.float32)
 
 
-def spread_kernel(chunks, x_ref, tr_ref, ti_ref, th_ref, tl_ref, o_ref, work_ref):
+def width_rows(chunk, chunks, owners, x_at, rows, target, tr_ref, ti_ref, v_ref):
+    values = []
+    for first in range(owners):
+        total = None
+        for second in range(chunks):
+            at = (first + owners * second) * HIGH
+            value = scaled((x_at(0, rows, at), x_at(1, rows, at)), *root(chunk * second, chunks, -1.0))
+            total = value if total is None else add(total, value)
+        values.append(scaled(total, *root(chunk * first, LOW, -1.0)))
+    for owner, (real, imaginary) in enumerate(butterfly(values, -1.0)):
+        k = chunks * owner + chunk
+        turn_real, turn_imaginary = tr_ref[k:k + 1, :], ti_ref[k:k + 1, :]
+        v_ref[owner, target, :HIGH] = real * turn_real - imaginary * turn_imaginary
+        v_ref[owner, target, HIGH:] = real * turn_imaginary + imaginary * turn_real
+
+
+def width_dense(step, th_ref, tl_ref, v_ref, put):
+    value = jnp.concatenate([v_ref[2 * step], v_ref[2 * step + 1]], axis=0)
+    high, low = split(value)
+    out = nt_dot(th_ref[...], high) + nt_dot(th_ref[...], low) + nt_dot(tl_ref[...], high)
+    for i in range(2):
+        for part in range(PARTS):
+            for side in range(2):
+                at = side * HIGH + part * PART
+                put(part, 2 * step + i, side, out[at:at + PART, i * HIGH:(i + 1) * HIGH])
+
+
+def spread_kernel(chunks, owners, x_ref, tr_ref, ti_ref, th_ref, tl_ref, o_ref, v_ref):
     def body(step, carry):
         rows = pl.ds(pl.multiple_of(step * 8, 8), 8)
-        values = [(x_ref[0, rows, g * HIGH:(g + 1) * HIGH], x_ref[1, rows, g * HIGH:(g + 1) * HIGH]) for g in range(LOW)]
-        for k, (real, imaginary) in enumerate(butterfly(values, -1.0)):
-            turn_real, turn_imaginary = tr_ref[k:k + 1, :], ti_ref[k:k + 1, :]
-            work_ref[k, rows, :HIGH] = real * turn_real - imaginary * turn_imaginary
-            work_ref[k, rows, HIGH:] = real * turn_imaginary + imaginary * turn_real
+        width_rows(0, chunks, owners, lambda side, r, at: x_ref[side, r, at:at + HIGH], rows, rows, tr_ref, ti_ref, v_ref)
         return carry
 
     lax.fori_loop(0, HIGH // 8, body, 0)
 
+    def put(part, owner, side, value):
+        o_ref[part, owner, 0, side] = value
+
     def dense(step, carry):
-        value = jnp.concatenate([work_ref[2 * step], work_ref[2 * step + 1]], axis=0)
-        high, low = split(value)
-        out = nt_dot(th_ref[...], high) + nt_dot(th_ref[...], low) + nt_dot(tl_ref[...], high)
-        for i in range(2):
-            k = 2 * step + i
-            owner, chunk = k // chunks, k % chunks
-            for part in range(PARTS):
-                for side in range(2):
-                    at = side * HIGH + part * PART
-                    o_ref[chunk * PARTS + part, owner, 0, side] = out[at:at + PART, i * HIGH:(i + 1) * HIGH]
-        return carry
-
-    lax.fori_loop(0, LOW // 2, dense, 0)
+        width_dense(step, th_ref, tl_ref, v_ref, put)
+        return carry
+
+    lax.fori_loop(0, owners // 2, dense, 0)
 
 
 def spread_width(field, chunks, owners, tables):
     _, height, _ = field.shape
     whole = lambda a: pl.BlockSpec(a.shape, lambda i: (0,) * a.ndim)
-    shape = (chunks * PARTS, owners, height // HIGH, 2, PART, HIGH)
+    shape = (PARTS, owners, height // HIGH, 2, PART, HIGH)
     return pl.pallas_call(
-        functools.partial(spread_kernel, chunks),
+        functools.partial(spread_kernel, chunks, owners),
         grid=(height // HIGH,),
         in_specs=[pl.BlockSpec((2, HIGH, N), lambda i: (0, i, 0))] + [whole(a) for a in tables],
         out_specs=pl.BlockSpec(shape[:2] + (1,) + shape[3:], lambda i: (0, 0, i, 0, 0, 0)),
         out_shape=jax.ShapeDtypeStruct(shape, jnp.float32),
-        scratch_shapes=[pltpu.VMEM((LOW, HIGH, 2 * HIGH), jnp.float32)],
+        scratch_shapes=[pltpu.VMEM((owners, HIGH, 2 * HIGH), jnp.float32)],
         compiler_params=pltpu.CompilerParams(vmem_limit_bytes=VMEM_LIMIT),
         name="spread",
     )(field, *tables)
 
 
-def line_kernel(chunks, owners, depths, scalars_ref, tr_ref, ti_ref, fh_ref, fl_ref, ih_ref, il_ref, sent_ref, back_ref,
-                buf, rbuf, lbuf, work_ref, self_f, send_f, recv_f, send_r, recv_r, send_l, recv_l, self_b, send_b, recv_b):
-    total = chunks * PARTS
+def line_kernel(chunks, owners, depths, outer, levels, scalars_ref, tr_ref, ti_ref, th_ref, tl_ref, fh_ref, fl_ref, ih_ref, il_ref,
+                sent_ref, x_ref, back_ref, buf, zbuf, stage, xbuf, v_ref, work_ref,
+                self_f, send_f, recv_f, send_r, recv_r, send_l, recv_l, self_b, send_b, recv_b, x_sem):
+    total = chunks * levels
     block = LOW // depths
     pieces = LOW // owners
+    ahead = max(1, levels - pieces)
+    halves_all = (chunks - 1) * pieces * 2
+    tall = HIGH // 2
     here, me = lax.axis_index("depth"), lax.axis_index("rows")
     last = depths - 1 - here
+    inner = jnp.minimum(here, 1) * jnp.minimum(last, 1)
+    mine = outer + (levels - outer) * inner
+
+    def active(t):
+        return t % levels < mine
+
+    def filled(t):
+        return t % levels < outer
+
+    def when(*conditions):
+        return pl.when(functools.reduce(jnp.logical_and, conditions))
+
+    def x_copy(h):
+        return pltpu.make_async_copy(x_ref.at[:, pl.ds((h % (2 * pieces)) * tall, tall), :], xbuf.at[h % 2], x_sem.at[h % 2])
+
+    for h in range(min(2, halves_all)):
+        x_copy(h).start()
 
     barrier = pltpu.get_barrier_semaphore()
     for step in range(1, owners):
@@ -405,15 +443,12 @@
 
     pl.semaphore_wait(barrier, owners - 1 + jnp.minimum(here, 1) + jnp.minimum(last, 1))
 
-    def own_copy(t):
-        return pltpu.make_async_copy(sent_ref.at[t, me], buf.at[t, pl.ds(me * pieces, pieces)], self_f.at[t])
-
-    def start_forward(t):
-        own_copy(t).start()
+    def forward_copies(source, t):
+        pltpu.make_async_copy(source.at[me], buf.at[t, pl.ds(me * pieces, pieces)], self_f.at[t]).start()
         for step in range(1, owners):
             peer = (me + step) % owners
             pltpu.make_async_remote_copy(
-                src_ref=sent_ref.at[t, peer],
+                src_ref=source.at[peer],
                 dst_ref=buf.at[t, pl.ds(me * pieces, pieces)],
                 send_sem=send_f.at[t],
                 recv_sem=recv_f.at[t],
@@ -421,6 +456,21 @@
                 device_id_type=MESH,
             ).start()
 
+    def start_forward(t):
+        group, part = t // levels, t % levels
+
+        @when(active(t), group == 0)
+        def _():
+            forward_copies(sent_ref.at[part], t)
+
+        @when(active(t), group > 0)
+        def _():
+            forward_copies(stage.at[(group + 1) % 2, part], t)
+
+    def arrived(t):
+        some = buf.at[t, pl.ds(me * pieces, pieces)]
+        return pltpu.make_async_copy(some, some, self_f.at[t])
+
     def others(t, sem):
         some = buf.at[t, pl.ds(0, pieces * (owners - 1))]
         return pltpu.make_async_copy(some, some, sem.at[t])
@@ -428,7 +478,7 @@
     def right_copy(t, q):
         return pltpu.make_async_remote_copy(
             src_ref=buf.at[t, pl.ds(q * block, block)],
-            dst_ref=rbuf.at[t, q - 1],
+            dst_ref=zbuf.at[t, q - here - 1],
             send_sem=send_r.at[t, q - 1],
             recv_sem=recv_r.at[t, q - 1],
             device_id=(here + 1, me),
@@ -438,17 +488,24 @@
     def left_copy(t, q):
         return pltpu.make_async_remote_copy(
             src_ref=buf.at[t, pl.ds(q * block, block)],
-            dst_ref=lbuf.at[t, q],
+            dst_ref=zbuf.at[t, depths - here + 1 + q],
             send_sem=send_l.at[t, q],
             recv_sem=recv_l.at[t, q],
             device_id=(here - 1, me),
             device_id_type=MESH,
         )
 
+    def landed(t, at, sem):
+        some = zbuf.at[t, at]
+        return pltpu.make_async_copy(some, some, sem)
+
+    def final_place(t):
+        return back_ref.at[(t // levels) * PARTS + t % levels]
+
     def final_copy(t, peer):
         return pltpu.make_async_remote_copy(
             src_ref=buf.at[t, here * block + peer],
-            dst_ref=back_ref.at[t, me],
+            dst_ref=final_place(t).at[me],
             send_sem=send_b.at[t],
             recv_sem=recv_b.at[t],
             device_id=(here, peer),
@@ -456,10 +513,10 @@
         )
 
     def final_own(t):
-        return pltpu.make_async_copy(buf.at[t, here * block + me], back_ref.at[t, me], self_b.at[t])
+        return pltpu.make_async_copy(buf.at[t, here * block + me], final_place(t).at[me], self_b.at[t])
 
     def finals(t, sem):
-        some = back_ref.at[t, pl.ds(0, owners - 1)]
+        some = final_place(t).at[pl.ds(0, owners - 1)]
         return pltpu.make_async_copy(some, some, sem.at[t])
 
     distance = scalars_ref[0].astype(jnp.float32) * 2.0 + 100.0
@@ -477,8 +534,8 @@
 
         lax.fori_loop(0, PART // 8, forward, 0)
 
-        column = me * chunks + t // PARTS
-        part = t % PARTS
+        column = me * chunks + t // levels
+        part = t % levels
         half = PART // 2
         slot = lax.broadcasted_iota(jnp.int32, (PART, HIGH), 0)
         turn = jnp.where(slot < half, half * part + slot, slot - half - half * (part + 1))
@@ -486,7 +543,7 @@
         inside_width = jnp.abs(across) < limit_width
         across_square = (across * (1.0 / N)) ** 2
         lanes = lax.broadcasted_iota(jnp.int32, (1, HIGH), 1) * LOW
-        group = 8
+        group = 16
 
         def middle(step, carry):
             taken = []
@@ -534,75 +591,139 @@
 
         lax.fori_loop(0, PART // 8, inverse, 0)
 
-    def merge(t, q, other, at):
-        def body(j, carry):
-            buf[t, q * block + j] += other[t, at, j]
+    def merge(t, q, at):
+        @pl.when(active(t))
+        def _():
+            def body(j, carry):
+                buf[t, q * block + j] += zbuf[t, at, j]
+                return carry
+
+            lax.fori_loop(0, block, body, 0)
+
+        if outer < levels:
+            @pl.when(jnp.logical_not(active(t)))
+            def _():
+                def body(j, carry):
+                    buf[t, q * block + j] = zbuf[t, at, j]
+                    return carry
+
+                lax.fori_loop(0, block, body, 0)
+
+    def width_tile(chunk, piece):
+        for half in range(2):
+            h = ((chunk - 1) * pieces + piece) * 2 + half
+            x_copy(h).wait()
+
+            def body(step, carry):
+                rows = pl.ds(pl.multiple_of(step * 8, 8), 8)
+                target = pl.ds(pl.multiple_of(step * 8 + half * tall, 8), 8)
+                width_rows(chunk, chunks, owners, lambda side, r, at: xbuf[half, side, r, at:at + HIGH], rows, target, tr_ref, ti_ref, v_ref)
+                return carry
+
+            lax.fori_loop(0, tall // 8, body, 0)
+
+            @pl.when(h + 2 < halves_all)
+            def _():
+                x_copy(h + 2).start()
+
+        def put(part, owner, side, value):
+            if isinstance(part, int) and part >= levels:
+                return
+            stage[(chunk + 1) % 2, part, owner, piece, side] = value
+
+        def dense(step, carry):
+            width_dense(step, th_ref, tl_ref, v_ref, put)
             return carry
 
-        lax.fori_loop(0, block, body, 0)
-
-    for t in range(min(AHEAD, total)):
+        lax.fori_loop(0, owners // 2, dense, 0)
+
+    def begin(t, carry):
         start_forward(t)
+        return carry
+
+    lax.fori_loop(0, min(ahead, total), begin, 0)
 
     def step(t, carry):
-        @pl.when(t + AHEAD < total)
+        @pl.when(t + ahead < total)
         def _():
-            start_forward(t + AHEAD)
-
-        @pl.when(t < total)
+            start_forward(t + ahead)
+
+        @when(t < total, active(t))
         def _():
-            own_copy(t).wait()
+            arrived(t).wait()
             others(t, recv_f).wait()
             columns(t)
 
         right = t - here
 
-        @pl.when(jnp.logical_and(right >= 0, right < total))
+        @when(right >= 0, right < total)
         def _():
             for q in range(depths - 1, 0, -1):
-                @pl.when(jnp.logical_and(here > 0, q >= here))
+                @when(here > 0, q >= here, jnp.logical_or(here > 1, filled(right)))
                 def _():
-                    right_copy(right, q).wait_recv()
-                    merge(right, q, rbuf, q - 1)
-
-                @pl.when(q > here)
+                    landed(right, q - here, recv_r.at[right, q - 1]).wait()
+                    merge(right, q, q - here)
+
+                @when(q > here, jnp.logical_or(here > 0, filled(right)))
                 def _():
                     right_copy(right, q).start()
 
         left = t - last
 
-        @pl.when(jnp.logical_and(left >= 0, left < total))
+        @when(left >= 0, left < total)
         def _():
             for q in range(depths - 1):
-                @pl.when(jnp.logical_and(last > 0, q <= here))
+                @when(last > 0, q <= here, jnp.logical_or(last > 1, filled(left)))
                 def _():
-                    left_copy(left, q).wait_recv()
-                    merge(left, q, lbuf, q)
-
-                @pl.when(q < here)
+                    landed(left, depths - here + q, recv_l.at[left, q]).wait()
+                    merge(left, q, depths - here + q)
+
+                @when(q < here, jnp.logical_or(last > 0, filled(left)))
                 def _():
                     left_copy(left, q).start()
 
         done = t - jnp.maximum(here, last)
 
-        @pl.when(jnp.logical_and(done >= 0, done < total))
+        @when(done >= 0, done < total)
         def _():
             final_own(done).start()
             for step in range(1, owners):
                 final_copy(done, (me + step) % owners).start()
 
+        group, piece = t // levels, t % levels
+        for chunk in range(1, chunks):
+            @when(group == chunk - 1, piece < pieces)
+            def _():
+                if chunk > 2:
+                    @pl.when(piece == 0)
+                    def _():
+                        def free(part, carry):
+                            @pl.when(active(part))
+                            def _():
+                                others((chunk - 2) * levels + part, send_f).wait()
+
+                            return carry
+
+                        lax.fori_loop(0, levels, free, 0)
+                width_tile(chunk, piece)
+
         return carry
 
     lax.fori_loop(0, total + depths - 1, step, 0)
 
     def finish(t, carry):
-        others(t, send_f).wait()
+        group = t // levels
+
+        @when(active(t), jnp.logical_or(group == 0, group + 2 >= chunks))
+        def _():
+            others(t, send_f).wait()
+
         for q in range(1, depths):
-            @pl.when(q > here)
+            @when(q > here, jnp.logical_or(here > 0, filled(t)))
             def _():
                 right_copy(t, q).wait_send()
         for q in range(depths - 1):
-            @pl.when(q < here)
+            @when(q < here, jnp.logical_or(last > 0, filled(t)))
             def _():
                 left_copy(t, q).wait_send()
         final_own(t).wait()
@@ -613,31 +734,35 @@
     lax.fori_loop(0, total, finish, 0)
 
 
-def line(sent, scalars, tables, chunks, owners, depths):
-    total = chunks * PARTS
+def line(sent, field, scalars, tables, chunks, owners, depths, outer, levels):
+    total = chunks * levels
     block = LOW // depths
+    pieces = LOW // owners
     vmem = pl.BlockSpec(memory_space=pltpu.VMEM)
     hbm = pl.BlockSpec(memory_space=pl.ANY)
     dma = pltpu.SemaphoreType.DMA
     tile = (2, PART, HIGH)
     return pl.pallas_call(
-        functools.partial(line_kernel, chunks, owners, depths),
-        in_specs=[pl.BlockSpec(memory_space=pltpu.SMEM)] + [vmem] * len(tables) + [hbm],
+        functools.partial(line_kernel, chunks, owners, depths, outer, levels),
+        in_specs=[pl.BlockSpec(memory_space=pltpu.SMEM)] + [vmem] * len(tables) + [hbm, hbm],
         out_specs=hbm,
-        out_shape=jax.ShapeDtypeStruct((total, owners) + tile, jnp.float32),
+        out_shape=jax.ShapeDtypeStruct((chunks * PARTS, owners) + tile, jnp.float32),
         scratch_shapes=[
             pltpu.VMEM((total, LOW) + tile, jnp.float32),
-            pltpu.VMEM((total, depths - 1, block) + tile, jnp.float32),
-            pltpu.VMEM((total, depths - 1, block) + tile, jnp.float32),
+            pltpu.VMEM((total, depths + 1, block) + tile, jnp.float32),
+            pltpu.VMEM((2, levels, owners, pieces) + tile, jnp.float32),
+            pltpu.VMEM((2, 2, HIGH // 2, N), jnp.float32),
+            pltpu.VMEM((owners, HIGH, 2 * HIGH), jnp.float32),
             pltpu.VMEM((LOW,) + tile, jnp.float32),
             dma((total,)), dma((total,)), dma((total,)),
             dma((total, depths - 1)), dma((total, depths - 1)),
             dma((total, depths - 1)), dma((total, depths - 1)),
             dma((total,)), dma((total,)), dma((total,)),
+            dma((2,)),
         ],
-        compiler_params=pltpu.CompilerParams(vmem_limit_bytes=VMEM_LIMIT, collective_id=0, has_side_effects=True),
+        compiler_params=pltpu.CompilerParams(vmem_limit_bytes=LINE_VMEM, collective_id=0, has_side_effects=True),
         name="line",
-    )(scalars, *tables, sent)
+    )(scalars, *tables, sent, field)
 
 
 def gather_kernel(chunks, in_ref, tr_ref, ti_ref, th_ref, tl_ref, o_ref, work_ref):
@@ -691,8 +816,10 @@
     turn_back = twiddles(1.0, scale / math.sqrt(depths))
     limits = (jnp.sum(band_mask[0], axis=-1) + 1) // 2
     scalars = jnp.stack([depth_index[0], limits[0], limits[1]]).astype(jnp.int32)
-    sent = spread_width(field, chunks, owners, turn + halves(forward[order]))
-    parts = line(sent, scalars, turn + halves(forward.T) + halves(backward.T), chunks, owners, depths)
+    wide = halves(forward[order])
+    sent = spread_width(field, chunks, owners, turn + wide)
+    tables = turn + wide + halves(forward.T) + halves(backward.T)
+    parts = line(sent, field, scalars, tables, chunks, owners, depths, PARTS, PARTS)
     return gather_width(parts, chunks, turn_back + halves(backward.T[order]))
 
 

time: 354 us -> 326 us (0.921)
  Pallas kernels: 352 us -> 324 us
    pallas_call x2, Pallas kernels: 342 us -> 314 us  [the longest x1 303 us: line(): pl.pallas_call(functools.partial(line_kernel, chunks, owners, depths, out...]
where the time goes in v1:
time: 326 us
  Pallas kernels  324 us (99%)
    pallas_call x1, Pallas kernels, line(): pl.pallas_call(functools.partial(line_kernel, chunks, owners, depths, out...  303 us
    pallas_call x1, Pallas kernels, spread_width(): pl.pallas_call(functools.partial(spread_kernel, chunks, owners), grid=(he...  11.1 us
    pallas_call x1, Pallas kernels, gather_width(): pl.pallas_call(functools.partial(gather_kernel, chunks), in_specs=[vmem]...  9.66 us

profile of v1, /device:TPU:0, one launch (start us, length us, event | category | flops | bytes accessed | tf_op | source)
XLA Modules:
  0.0 326.0 jit_solution(2770501454284941534)
XLA Ops:
  0.7 0.9 reduce_sum.9
  1.6 0.6 pad_add_fusion.scalars_ref
  2.2 11.1 %spread.1.sent_ref = f32[8,8,4,2,16,128]{5,4,3,2,1,0:T(8,128)} custom-call(f32[2,512,4096]{2,1,0:T(8,128)} %bitcast.1, f32[32,128]{1,0:T(8,128)} %constant.36.clone.tr_ref, f32[32,128]{1,0:T(8,128)} %constant.37.clone.ti_ref, bf16[256,256]{1,0:T(8,128)(2,1)} %constant.40.clone.th_ref, bf16[256,256]{1,0:T(8,128)(2,1)} %constant.41.clone.tl_ref), custom_call_target="tpu_custom_call" | custom-call | tf_op jit(solution)/shard_map/spread/pallas_call | solution.py:391
  13.3 303.0 %line.1.in_ref = f32[32,8,2,16,128]{4,3,2,1,0:T(8,128)} custom-call(s32[3]{0:T(128)} %pad_add_fusion.scalars_ref, f32[32,128]{1,0:T(8,128)} %constant.36.clone.tr_ref, f32[32,128]{1,0:T(8,128)} %constant.37.clone.ti_ref, bf16[256,256]{1,0:T(8,128)(2,1)} %constant.40.clone.th_ref, bf16[256,256]{1,0:T(8,128)(2,1)} %constant.41.clone.tl_ref, ...), custom_call_target="tpu_custom_call" | custom-call | tf_op jit(solution)/shard_map/line/pallas_call | solution.py:745
  316.3 9.7 %gather.1 = f32[2,128,4096]{2,1,0:T(8,128)} custom-call(f32[32,8,2,16,128]{4,3,2,1,0:T(8,128)} %line.1.in_ref, f32[32,128]{1,0:T(8,128)} %constant.38.clone.tr_ref, f32[32,128]{1,0:T(8,128)} %constant.39.clone.ti_ref, bf16[256,256]{1,0:T(8,128)(2,1)} %constant.40.clone.th_ref, bf16[256,256]{1,0:T(8,128)(2,1)} %constant.41.clone.tl_ref), custom_call_target="tpu_custom_call" | custom-call | tf_op jit(solution)/shard_map/gather/pallas_call | solution.py:797
  (1 shorter events, 0.0 us)

commit v2 on v1

--- a/solution.py
+++ b/solution.py
@@ -320,6 +320,7 @@
 PART = 16
 PARTS = HIGH // PART
 LINE_VMEM = 62 * 1024 * 1024
+VARIANTS = ((5, 6), (6, 7), (6, 8), (7, 7), (7, 8), (8, 8))
 
 
 def slots():
@@ -366,7 +367,41 @@
                 put(part, 2 * step + i, side, out[at:at + PART, i * HIGH:(i + 1) * HIGH])
 
 
-def spread_kernel(chunks, owners, x_ref, tr_ref, ti_ref, th_ref, tl_ref, o_ref, v_ref):
+def spread_kernel(chunks, owners, depths, depth_ref, mask_ref, x_ref, tr_ref, ti_ref, th_ref, tl_ref, o_ref, scalars_ref, choice_ref,
+                  v_ref, limit_ref, landing, send, recv):
+    here, me = lax.axis_index("depth"), lax.axis_index("rows")
+    tile = pl.program_id(0)
+
+    def limit_copy(step):
+        return pltpu.make_async_remote_copy(
+            src_ref=limit_ref,
+            dst_ref=landing.at[here],
+            send_sem=send,
+            recv_sem=recv,
+            device_id=((here + step) % depths, me),
+            device_id_type=MESH,
+        )
+
+    def sum_of_limits(sem):
+        some = landing.at[pl.ds(0, depths - 1)]
+        return pltpu.make_async_copy(some, some, sem)
+
+    @pl.when(tile == 0)
+    def _():
+        barrier = pltpu.get_barrier_semaphore()
+        for step in range(1, depths):
+            pl.semaphore_signal(barrier, inc=1, device_id=((here + step) % depths, me), device_id_type=MESH)
+        ones = mask_ref[0].astype(jnp.float32)
+        height, width = [(jnp.sum(ones[side:side + 1, :]) + 1.0) * 0.5 for side in range(2)]
+        scalars_ref[0] = depth_ref[0]
+        scalars_ref[1] = height.astype(jnp.int32)
+        scalars_ref[2] = width.astype(jnp.int32)
+        limit_ref[...] = jnp.full(limit_ref.shape, width)
+        landing[here] = jnp.full(limit_ref.shape, width)
+        pl.semaphore_wait(barrier, depths - 1)
+        for step in range(1, depths):
+            limit_copy(step).start()
+
     def body(step, carry):
         rows = pl.ds(pl.multiple_of(step * 8, 8), 8)
         width_rows(0, chunks, owners, lambda side, r, at: x_ref[side, r, at:at + HIGH], rows, rows, tr_ref, ti_ref, v_ref)
@@ -381,23 +416,48 @@
         width_dense(step, th_ref, tl_ref, v_ref, put)
         return carry
 
-    lax.fori_loop(0, owners // 2, dense, 0)
-
-
-def spread_width(field, chunks, owners, tables):
+    lax.fori_loop(0, owners // 2, dense, 0, unroll=True)
+
+    @pl.when(tile == pl.num_programs(0) - 1)
+    def _():
+        sum_of_limits(recv).wait()
+        sum_of_limits(send).wait()
+        widths = [jnp.max(landing[q]) for q in range(depths)]
+        outer, most = jnp.maximum(widths[0], widths[-1]), functools.reduce(jnp.maximum, widths)
+        reach = LOW * PART // 2
+        missed, fits = jnp.int32(0), jnp.bool_(False)
+        for a, b in VARIANTS[:-1]:
+            fits = jnp.logical_or(fits, jnp.logical_and(outer <= a * reach, most <= b * reach))
+            missed = missed + jnp.where(fits, 0, 1)
+        choice_ref[0] = missed
+        choice_ref[1] = sum(jnp.where(most > part * reach, 1, 0) for part in range(PARTS))
+
+
+def spread_width(field, depth_index, band_mask, chunks, owners, depths, tables):
     _, height, _ = field.shape
     whole = lambda a: pl.BlockSpec(a.shape, lambda i: (0,) * a.ndim)
+    smem = pl.BlockSpec(memory_space=pltpu.SMEM)
     shape = (PARTS, owners, height // HIGH, 2, PART, HIGH)
     return pl.pallas_call(
-        functools.partial(spread_kernel, chunks, owners),
+        functools.partial(spread_kernel, chunks, owners, depths),
         grid=(height // HIGH,),
-        in_specs=[pl.BlockSpec((2, HIGH, N), lambda i: (0, i, 0))] + [whole(a) for a in tables],
-        out_specs=pl.BlockSpec(shape[:2] + (1,) + shape[3:], lambda i: (0, 0, i, 0, 0, 0)),
-        out_shape=jax.ShapeDtypeStruct(shape, jnp.float32),
-        scratch_shapes=[pltpu.VMEM((owners, HIGH, 2 * HIGH), jnp.float32)],
-        compiler_params=pltpu.CompilerParams(vmem_limit_bytes=VMEM_LIMIT),
+        in_specs=[smem, pl.BlockSpec(memory_space=pltpu.VMEM), pl.BlockSpec((2, HIGH, N), lambda i: (0, i, 0))] + [whole(a) for a in tables],
+        out_specs=[
+            pl.BlockSpec(shape[:2] + (1,) + shape[3:], lambda i: (0, 0, i, 0, 0, 0)),
+            smem,
+            smem,
+        ],
+        out_shape=[jax.ShapeDtypeStruct(shape, jnp.float32), jax.ShapeDtypeStruct((3,), jnp.int32), jax.ShapeDtypeStruct((2,), jnp.int32)],
+        scratch_shapes=[
+            pltpu.VMEM((owners, HIGH, 2 * HIGH), jnp.float32),
+            pltpu.VMEM((8, HIGH), jnp.float32),
+            pltpu.VMEM((depths, 8, HIGH), jnp.float32),
+            pltpu.SemaphoreType.DMA,
+            pltpu.SemaphoreType.DMA,
+        ],
+        compiler_params=pltpu.CompilerParams(vmem_limit_bytes=VMEM_LIMIT, collective_id=0, has_side_effects=True),
         name="spread",
-    )(field, *tables)
+    )(depth_index, band_mask, field, *tables)
 
 
 def line_kernel(chunks, owners, depths, outer, levels, scalars_ref, tr_ref, ti_ref, th_ref, tl_ref, fh_ref, fl_ref, ih_ref, il_ref,
@@ -734,7 +794,8 @@
     lax.fori_loop(0, total, finish, 0)
 
 
-def line(sent, field, scalars, tables, chunks, owners, depths, outer, levels):
+def line(variant, chunks, owners, depths, sent, field, scalars, *tables):
+    outer, levels = VARIANTS[variant]
     total = chunks * levels
     block = LOW // depths
     pieces = LOW // owners
@@ -760,16 +821,20 @@
             dma((total,)), dma((total,)), dma((total,)),
             dma((2,)),
         ],
-        compiler_params=pltpu.CompilerParams(vmem_limit_bytes=LINE_VMEM, collective_id=0, has_side_effects=True),
-        name="line",
+        compiler_params=pltpu.CompilerParams(vmem_limit_bytes=LINE_VMEM, collective_id=1 + variant, has_side_effects=True),
     )(scalars, *tables, sent, field)
 
 
-def gather_kernel(chunks, in_ref, tr_ref, ti_ref, th_ref, tl_ref, o_ref, work_ref):
+def gather_kernel(chunks, levels_ref, in_ref, tr_ref, ti_ref, th_ref, tl_ref, o_ref, work_ref):
+    levels = levels_ref[1]
+
     def dense(k, carry):
         owner, chunk = k // chunks, k % chunks
         sides = [
-            jnp.concatenate([in_ref[chunk * PARTS + part, owner, side] for part in range(PARTS)], axis=0).T for side in range(2)
+            jnp.concatenate([
+                jnp.where(part < levels, in_ref[chunk * PARTS + part, owner, side], 0.0) for part in range(PARTS)
+            ], axis=0).T
+            for side in range(2)
         ]
         high, low = split(jnp.concatenate(sides, axis=1))
         out = dot(high, th_ref[...]) + dot(low, th_ref[...]) + dot(high, tl_ref[...])
@@ -792,17 +857,17 @@
     lax.fori_loop(0, HIGH // 8, body, 0)
 
 
-def gather_width(parts, chunks, tables):
+def gather_width(parts, levels, chunks, tables):
     vmem = pl.BlockSpec(memory_space=pltpu.VMEM)
     return pl.pallas_call(
         functools.partial(gather_kernel, chunks),
-        in_specs=[vmem] * (1 + len(tables)),
+        in_specs=[pl.BlockSpec(memory_space=pltpu.SMEM)] + [vmem] * (1 + len(tables)),
         out_specs=vmem,
         out_shape=jax.ShapeDtypeStruct((2, HIGH, N), jnp.float32),
         scratch_shapes=[pltpu.VMEM((LOW, 2, HIGH, HIGH), jnp.float32)],
         compiler_params=pltpu.CompilerParams(vmem_limit_bytes=VMEM_LIMIT),
         name="gather",
-    )(parts, *tables)
+    )(levels, parts, *tables)
 
 
 def fused(target, depth_index, band_mask):
@@ -814,13 +879,12 @@
     order = both(slots())
     turn = twiddles(-1.0, scale)
     turn_back = twiddles(1.0, scale / math.sqrt(depths))
-    limits = (jnp.sum(band_mask[0], axis=-1) + 1) // 2
-    scalars = jnp.stack([depth_index[0], limits[0], limits[1]]).astype(jnp.int32)
     wide = halves(forward[order])
-    sent = spread_width(field, chunks, owners, turn + wide)
+    sent, scalars, choice = spread_width(field, depth_index, band_mask, chunks, owners, depths, turn + wide)
+    choices = [functools.partial(line, i, chunks, owners, depths) for i in range(len(VARIANTS))]
     tables = turn + wide + halves(forward.T) + halves(backward.T)
-    parts = line(sent, field, scalars, tables, chunks, owners, depths, PARTS, PARTS)
-    return gather_width(parts, chunks, turn_back + halves(backward.T[order]))
+    parts = lax.switch(choice[0], choices, sent, field, scalars, *tables)
+    return gather_width(parts, choice, chunks, turn_back + halves(backward.T[order]))
 
 
 def solution(mesh):

time: 326 us -> 234 us (0.72)
  Pallas kernels: 324 us -> 232 us
    pallas_call x1, Pallas kernels: 303 us -> 207 us  [line(): pl.pallas_call(functools.partial(line_kernel, chunks, owners, depths, out...]
    pallas_call x2, Pallas kernels: 20.8 us -> 25.8 us  [the longest x1 16.1 us: spread_width(): pl.pallas_call(functools.partial(spread_kernel, chunks, owners, depths),...]
where the time goes in v2:
time: 234 us
  Pallas kernels  232 us (99%)
    pallas_call x1, Pallas kernels, line(): pl.pallas_call(functools.partial(line_kernel, chunks, owners, depths, out...  207 us
    pallas_call x1, Pallas kernels, spread_width(): pl.pallas_call(functools.partial(spread_kernel, chunks, owners, depths),...  16.1 us
    pallas_call x1, Pallas kernels, gather_width(): pl.pallas_call(functools.partial(gather_kernel, chunks), in_specs=[pl.Blo...  9.68 us

profile of v2, /device:TPU:0, one launch (start us, length us, event | category | flops | bytes accessed | tf_op | source)
XLA Modules:
  0.0 234.0 jit_solution(8718303190785967599)
XLA Ops:
  0.7 0.0 copy-start
  0.7 0.0 copy-start.1
  0.7 0.0 copy-start.2
  0.7 0.0 copy-start.3
  0.7 0.0 copy-start.4
  0.7 0.0 copy-start.5
  0.7 0.0 copy-start.6
  0.7 0.0 copy-start.7
  0.8 16.1 %spread.1 = (f32[8,8,4,2,16,128]{5,4,3,2,1,0:T(8,128)}, s32[3]{0:T(128)S(1)}, s32[2]{0:T(128)}) custom-call(s32[1]{0:T(128)S(6)} %copy.22.depth_ref, s32[1,2,4096]{2,1,0:T(2,128)} %mask_ref.1, f32[2,512,4096]{2,1,0:T(8,128)} %bitcast.3, f32[32,128]{1,0:T(8,128)} %constant.26.clone.tr_ref, f32[32,128]{1,0:T(8,128)} %constant.27.clone.ti_ref, ...), custom_call_target="tpu_custom_call" | custom-call | tf_op jit(solution)/shard_map/spread/pallas_call | solution.py:441
  17.5 0.0 copy-done
  17.5 0.0 copy-done.1
  17.5 0.0 copy-done.2
  17.5 0.0 copy-done.3
  17.5 0.0 copy-done.4
  17.5 0.0 copy-done.5
  17.5 0.0 copy-done.6
  17.5 0.0 copy-done.7
  17.5 206.8 %conditional.1 = (f32[32,8,2,16,128]{4,3,2,1,0:T(8,128)}) conditional(s32[]{:T(128)} %bitcast.1, (s32[3]{0:T(128)S(1)}, f32[32,128]{1,0:T(8,128)S(1)}, f32[32,128]{1,0:T(8,128)S(1)}, bf16[256,256]{1,0:T(8,128)(2,1)S(1)}, bf16[256,256]{1,0:T(8,128)(2,1)S(1)}, /*index=5*/bf16[256,256]{1,0:T(8,128)(2,1)S(1)}, ...), branch_computations={%region_0.0_spmd, %region_1.0_spmd, %region_2.0_spmd, %region_3.0_... | conditional | bytes 8 | solution.py:886
  17.6 206.5 %branch_0_fun.1 = f32[32,8,2,16,128]{4,3,2,1,0:T(8,128)} custom-call(s32[3]{0:T(128)S(1)} %get-tuple-element.98.scalars_ref, f32[32,128]{1,0:T(8,128)S(1)} %get-tuple-element.120.tr_ref, f32[32,128]{1,0:T(8,128)S(1)} %get-tuple-element.144.ti_ref, bf16[256,256]{1,0:T(8,128)(2,1)S(1)} %get-tuple-element.146.th_ref, ...), custom_call_target="tpu_custom_call" | custom-call | tf_op jit(solution)/shard_map/cond/branch_0_fun/pallas_call | solution.py:806
  224.3 9.7 %gather.1 = f32[2,128,4096]{2,1,0:T(8,128)} custom-call(s32[2]{0:T(128)} %get-tuple-element.213.levels_ref, f32[32,8,2,16,128]{4,3,2,1,0:T(8,128)} %get-tuple-element.216.in_ref, f32[32,128]{1,0:T(8,128)} %constant.28.clone.tr_ref, f32[32,128]{1,0:T(8,128)} %constant.29.clone.ti_ref, bf16[256,256]{1,0:T(8,128)(2,1)S(1)} %copy-done.1, ...), custom_call_target="tpu_custom_call" | custom-call | tf_op jit(solution)/shard_map/gather/pallas_call | solution.py:862
Async XLA Ops:
  0.7 16.8 %copy-start = (bf16[256,256]{1,0:T(8,128)(2,1)S(1)}, bf16[256,256]{1,0:T(8,128)(2,1)}, u32[]{:S(2)}) copy-start(bf16[256,256]{1,0:T(8,128)(2,1)} %constant.31.clone.tl_ref) | copy-start | bytes 393220
  0.7 16.8 %copy-start.1 = (bf16[256,256]{1,0:T(8,128)(2,1)S(1)}, bf16[256,256]{1,0:T(8,128)(2,1)}, u32[]{:S(2)}) copy-start(bf16[256,256]{1,0:T(8,128)(2,1)} %constant.30.clone.th_ref) | copy-start | bytes 393220
  0.7 16.8 %copy-start.2 = (bf16[256,256]{1,0:T(8,128)(2,1)S(1)}, bf16[256,256]{1,0:T(8,128)(2,1)}, u32[]{:S(2)}) copy-start(bf16[256,256]{1,0:T(8,128)(2,1)} %constant.35.clone) | copy-start | bytes 393220
  0.7 16.8 %copy-start.3 = (bf16[256,256]{1,0:T(8,128)(2,1)S(1)}, bf16[256,256]{1,0:T(8,128)(2,1)}, u32[]{:S(2)}) copy-start(bf16[256,256]{1,0:T(8,128)(2,1)} %constant.34.clone) | copy-start | bytes 393220
  0.7 16.8 %copy-start.4 = (bf16[256,256]{1,0:T(8,128)(2,1)S(1)}, bf16[256,256]{1,0:T(8,128)(2,1)}, u32[]{:S(2)}) copy-start(bf16[256,256]{1,0:T(8,128)(2,1)} %constant.33.clone) | copy-start | bytes 393220
  0.7 16.8 %copy-start.5 = (bf16[256,256]{1,0:T(8,128)(2,1)S(1)}, bf16[256,256]{1,0:T(8,128)(2,1)}, u32[]{:S(2)}) copy-start(bf16[256,256]{1,0:T(8,128)(2,1)} %constant.32.clone) | copy-start | bytes 393220
  0.7 16.8 %copy-start.6 = (f32[32,128]{1,0:T(8,128)S(1)}, f32[32,128]{1,0:T(8,128)}, u32[]{:S(2)}) copy-start(f32[32,128]{1,0:T(8,128)} %constant.27.clone.ti_ref) | copy-start | bytes 49156
  0.7 16.8 %copy-start.7 = (f32[32,128]{1,0:T(8,128)S(1)}, f32[32,128]{1,0:T(8,128)}, u32[]{:S(2)}) copy-start(f32[32,128]{1,0:T(8,128)} %constant.26.clone.tr_ref) | copy-start | bytes 49156

commit v3 on v2

--- a/solution.py
+++ b/solution.py
@@ -320,7 +320,9 @@
 PART = 16
 PARTS = HIGH // PART
 LINE_VMEM = 62 * 1024 * 1024
-VARIANTS = ((5, 6), (6, 7), (6, 8), (7, 7), (7, 8), (8, 8))
+HOLD = 8
+SLACK = 4
+VARIANTS = ((5, 6), (5, 7), (6, 7), (6, 8), (7, 8), (8, 8))
 
 
 def slots():
@@ -697,6 +699,11 @@
 
         lax.fori_loop(0, owners // 2, dense, 0)
 
+    def finals_by(t):
+        ready = t - jnp.maximum(here, last) - SLACK + 1
+        late = jnp.minimum(jnp.maximum(t - (total - ahead) + 1, 0), 1)
+        return jnp.minimum(jnp.maximum(ready - HOLD * (1 - late), 0), total)
+
     def begin(t, carry):
         start_forward(t)
         return carry
@@ -714,7 +721,7 @@
             others(t, recv_f).wait()
             columns(t)
 
-        right = t - here
+        right = t - here - SLACK * jnp.minimum(here, 1)
 
         @when(right >= 0, right < total)
         def _():
@@ -728,7 +735,7 @@
                 def _():
                     right_copy(right, q).start()
 
-        left = t - last
+        left = t - last - SLACK * jnp.minimum(last, 1)
 
         @when(left >= 0, left < total)
         def _():
@@ -742,13 +749,13 @@
                 def _():
                     left_copy(left, q).start()
 
-        done = t - jnp.maximum(here, last)
-
-        @when(done >= 0, done < total)
-        def _():
+        def send_final(done, carry):
             final_own(done).start()
             for step in range(1, owners):
                 final_copy(done, (me + step) % owners).start()
+            return carry
+
+        lax.fori_loop(finals_by(t - 1), finals_by(t), send_final, 0)
 
         group, piece = t // levels, t % levels
         for chunk in range(1, chunks):
@@ -769,7 +776,7 @@
 
         return carry
 
-    lax.fori_loop(0, total + depths - 1, step, 0)
+    lax.fori_loop(0, total + depths - 1 + SLACK, step, 0)
 
     def finish(t, carry):
         group = t // levels
@@ -825,46 +832,75 @@
     )(scalars, *tables, sent, field)
 
 
-def gather_kernel(chunks, levels_ref, in_ref, tr_ref, ti_ref, th_ref, tl_ref, o_ref, work_ref):
+def gather_kernel(chunks, owners, levels_ref, in_ref, tr_ref, ti_ref, th_ref, tl_ref, out_ref, held_ref, work_ref, o_ref, in_sem, out_sem):
     levels = levels_ref[1]
-
-    def dense(k, carry):
-        owner, chunk = k // chunks, k % chunks
-        sides = [
-            jnp.concatenate([
-                jnp.where(part < levels, in_ref[chunk * PARTS + part, owner, side], 0.0) for part in range(PARTS)
-            ], axis=0).T
-            for side in range(2)
-        ]
-        high, low = split(jnp.concatenate(sides, axis=1))
-        out = dot(high, th_ref[...]) + dot(low, th_ref[...]) + dot(high, tl_ref[...])
-        real, imaginary = out[:, :HIGH], out[:, HIGH:]
-        turn_real, turn_imaginary = tr_ref[pl.ds(k, 1), :], ti_ref[pl.ds(k, 1), :]
-        work_ref[k, 0] = real * turn_real - imaginary * turn_imaginary
-        work_ref[k, 1] = real * turn_imaginary + imaginary * turn_real
-        return carry
-
-    lax.fori_loop(0, LOW, dense, 0, unroll=4)
+    lines = 8
+
+    def in_copy(chunk):
+        some = pl.ds(chunk * PARTS, PARTS)
+        return pltpu.make_async_copy(in_ref.at[some], held_ref.at[some], in_sem.at[chunk])
+
+    def out_copy(step):
+        rows = pl.ds(pl.multiple_of(step * lines, lines), lines)
+        return pltpu.make_async_copy(o_ref.at[:, rows, :], out_ref.at[:, rows, :], out_sem.at[step])
+
+    for chunk in range(chunks):
+        in_copy(chunk).start()
+
+    for chunk in range(chunks):
+        in_copy(chunk).wait()
+
+        def dense(owner, carry):
+            k = owner * chunks + chunk
+            sides = [
+                jnp.concatenate([
+                    jnp.where(part < levels, held_ref[chunk * PARTS + part, owner, side], 0.0) for part in range(PARTS)
+                ], axis=0).T
+                for side in range(2)
+            ]
+            high, low = split(jnp.concatenate(sides, axis=1))
+            out = dot(high, th_ref[...]) + dot(low, th_ref[...]) + dot(high, tl_ref[...])
+            real, imaginary = out[:, :HIGH], out[:, HIGH:]
+            turn_real, turn_imaginary = tr_ref[pl.ds(k, 1), :], ti_ref[pl.ds(k, 1), :]
+            work_ref[k, 0] = real * turn_real - imaginary * turn_imaginary
+            work_ref[k, 1] = real * turn_imaginary + imaginary * turn_real
+            return carry
+
+        lax.fori_loop(0, owners, dense, 0, unroll=4)
 
     def body(step, carry):
-        rows = pl.ds(pl.multiple_of(step * 8, 8), 8)
+        rows = pl.ds(pl.multiple_of(step * lines, lines), lines)
         values = [(work_ref[k, 0, rows, :], work_ref[k, 1, rows, :]) for k in range(LOW)]
         for j, (real, imaginary) in enumerate(butterfly(values, 1.0)):
             o_ref[0, rows, j * HIGH:(j + 1) * HIGH] = real
             o_ref[1, rows, j * HIGH:(j + 1) * HIGH] = imaginary
-        return carry
-
-    lax.fori_loop(0, HIGH // 8, body, 0)
-
-
-def gather_width(parts, levels, chunks, tables):
+        out_copy(step).start()
+        return carry
+
+    lax.fori_loop(0, HIGH // lines, body, 0)
+
+    def flush(step, carry):
+        out_copy(step).wait()
+        return carry
+
+    lax.fori_loop(0, HIGH // lines, flush, 0)
+
+
+def gather_width(parts, levels, chunks, owners, tables):
     vmem = pl.BlockSpec(memory_space=pltpu.VMEM)
+    hbm = pl.BlockSpec(memory_space=pl.ANY)
     return pl.pallas_call(
-        functools.partial(gather_kernel, chunks),
-        in_specs=[pl.BlockSpec(memory_space=pltpu.SMEM)] + [vmem] * (1 + len(tables)),
-        out_specs=vmem,
+        functools.partial(gather_kernel, chunks, owners),
+        in_specs=[pl.BlockSpec(memory_space=pltpu.SMEM), hbm] + [vmem] * len(tables),
+        out_specs=hbm,
         out_shape=jax.ShapeDtypeStruct((2, HIGH, N), jnp.float32),
-        scratch_shapes=[pltpu.VMEM((LOW, 2, HIGH, HIGH), jnp.float32)],
+        scratch_shapes=[
+            pltpu.VMEM(parts.shape, jnp.float32),
+            pltpu.VMEM((LOW, 2, HIGH, HIGH), jnp.float32),
+            pltpu.VMEM((2, HIGH, N), jnp.float32),
+            pltpu.SemaphoreType.DMA((chunks,)),
+            pltpu.SemaphoreType.DMA((HIGH // 8,)),
+        ],
         compiler_params=pltpu.CompilerParams(vmem_limit_bytes=VMEM_LIMIT),
         name="gather",
     )(levels, parts, *tables)
@@ -884,7 +920,7 @@
     choices = [functools.partial(line, i, chunks, owners, depths) for i in range(len(VARIANTS))]
     tables = turn + wide + halves(forward.T) + halves(backward.T)
     parts = lax.switch(choice[0], choices, sent, field, scalars, *tables)
-    return gather_width(parts, choice, chunks, turn_back + halves(backward.T[order]))
+    return gather_width(parts, choice, chunks, owners, turn_back + halves(backward.T[order]))
 
 
 def solution(mesh):

time: 234 us -> 228 us (0.974)
  Pallas kernels: 232 us -> 226 us
    pallas_call x1, Pallas kernels: 207 us -> 202 us  [line(): pl.pallas_call(functools.partial(line_kernel, chunks, owners, depths, out...]
where the time goes in v3:
time: 228 us
  Pallas kernels  226 us (99%)
    pallas_call x1, Pallas kernels, line(): pl.pallas_call(functools.partial(line_kernel, chunks, owners, depths, out...  202 us
    pallas_call x1, Pallas kernels, spread_width(): pl.pallas_call(functools.partial(spread_kernel, chunks, owners, depths),...  16.1 us
    pallas_call x1, Pallas kernels, gather_width(): pl.pallas_call(functools.partial(gather_kernel, chunks, owners), in_specs...  8.17 us

profile of v3, /device:TPU:0, one launch (start us, length us, event | category | flops | bytes accessed | tf_op | source)
XLA Modules:
  0.0 228.1 jit_solution(10388359796711052043)
XLA Ops:
  0.7 0.0 copy-start
  0.7 0.0 copy-start.1
  0.7 0.0 copy-start.2
  0.7 0.0 copy-start.3
  0.7 0.0 copy-start.4
  0.7 0.0 copy-start.5
  0.7 0.0 copy-start.6
  0.7 0.0 copy-start.7
  0.8 16.1 %spread.1 = (f32[8,8,4,2,16,128]{5,4,3,2,1,0:T(8,128)}, s32[3]{0:T(128)S(1)}, s32[2]{0:T(128)}) custom-call(s32[1]{0:T(128)S(6)} %copy.22.depth_ref, s32[1,2,4096]{2,1,0:T(2,128)} %mask_ref.1, f32[2,512,4096]{2,1,0:T(8,128)} %bitcast.3, f32[32,128]{1,0:T(8,128)} %constant.26.clone.tr_ref, f32[32,128]{1,0:T(8,128)} %constant.27.clone.ti_ref, ...), custom_call_target="tpu_custom_call" | custom-call | tf_op jit(solution)/shard_map/spread/pallas_call | solution.py:443
  17.5 0.0 copy-done
  17.5 0.0 copy-done.1
  17.5 0.0 copy-done.2
  17.5 0.0 copy-done.3
  17.5 0.0 copy-done.4
  17.5 0.0 copy-done.5
  17.5 0.0 copy-done.6
  17.5 0.0 copy-done.7
  17.5 202.2 %conditional.1 = (f32[32,8,2,16,128]{4,3,2,1,0:T(8,128)}) conditional(s32[]{:T(128)} %bitcast.1, (s32[3]{0:T(128)S(1)}, f32[32,128]{1,0:T(8,128)S(1)}, f32[32,128]{1,0:T(8,128)S(1)}, bf16[256,256]{1,0:T(8,128)(2,1)S(1)}, bf16[256,256]{1,0:T(8,128)(2,1)S(1)}, /*index=5*/bf16[256,256]{1,0:T(8,128)(2,1)S(1)}, ...), branch_computations={%region_0.0_spmd, %region_1.0_spmd, %region_2.0_spmd, %region_3.0_... | conditional | bytes 8 | solution.py:922
  17.6 201.9 %branch_0_fun.1 = f32[32,8,2,16,128]{4,3,2,1,0:T(8,128)} custom-call(s32[3]{0:T(128)S(1)} %get-tuple-element.98.scalars_ref, f32[32,128]{1,0:T(8,128)S(1)} %get-tuple-element.120.tr_ref, f32[32,128]{1,0:T(8,128)S(1)} %get-tuple-element.144.ti_ref, bf16[256,256]{1,0:T(8,128)(2,1)S(1)} %get-tuple-element.146.th_ref, ...), custom_call_target="tpu_custom_call" | custom-call | tf_op jit(solution)/shard_map/cond/branch_0_fun/pallas_call | solution.py:813
  219.8 8.2 %gather.1 = f32[2,128,4096]{2,1,0:T(8,128)} custom-call(s32[2]{0:T(128)} %get-tuple-element.213.levels_ref, f32[32,8,2,16,128]{4,3,2,1,0:T(8,128)} %get-tuple-element.216.in_ref, f32[32,128]{1,0:T(8,128)} %constant.28.clone.tr_ref, f32[32,128]{1,0:T(8,128)} %constant.29.clone.ti_ref, bf16[256,256]{1,0:T(8,128)(2,1)S(1)} %copy-done.1, ...), custom_call_target="tpu_custom_call" | custom-call | tf_op jit(solution)/shard_map/gather/pallas_call | solution.py:892
Async XLA Ops:
  0.7 16.8 %copy-start = (bf16[256,256]{1,0:T(8,128)(2,1)S(1)}, bf16[256,256]{1,0:T(8,128)(2,1)}, u32[]{:S(2)}) copy-start(bf16[256,256]{1,0:T(8,128)(2,1)} %constant.31.clone.tl_ref) | copy-start | bytes 393220
  0.7 16.8 %copy-start.1 = (bf16[256,256]{1,0:T(8,128)(2,1)S(1)}, bf16[256,256]{1,0:T(8,128)(2,1)}, u32[]{:S(2)}) copy-start(bf16[256,256]{1,0:T(8,128)(2,1)} %constant.30.clone.th_ref) | copy-start | bytes 393220
  0.7 16.8 %copy-start.2 = (bf16[256,256]{1,0:T(8,128)(2,1)S(1)}, bf16[256,256]{1,0:T(8,128)(2,1)}, u32[]{:S(2)}) copy-start(bf16[256,256]{1,0:T(8,128)(2,1)} %constant.35.clone) | copy-start | bytes 393220
  0.7 16.8 %copy-start.3 = (bf16[256,256]{1,0:T(8,128)(2,1)S(1)}, bf16[256,256]{1,0:T(8,128)(2,1)}, u32[]{:S(2)}) copy-start(bf16[256,256]{1,0:T(8,128)(2,1)} %constant.34.clone) | copy-start | bytes 393220
  0.7 16.8 %copy-start.4 = (bf16[256,256]{1,0:T(8,128)(2,1)S(1)}, bf16[256,256]{1,0:T(8,128)(2,1)}, u32[]{:S(2)}) copy-start(bf16[256,256]{1,0:T(8,128)(2,1)} %constant.33.clone) | copy-start | bytes 393220
  0.7 16.8 %copy-start.5 = (bf16[256,256]{1,0:T(8,128)(2,1)S(1)}, bf16[256,256]{1,0:T(8,128)(2,1)}, u32[]{:S(2)}) copy-start(bf16[256,256]{1,0:T(8,128)(2,1)} %constant.32.clone) | copy-start | bytes 393220
  0.7 16.8 %copy-start.6 = (f32[32,128]{1,0:T(8,128)S(1)}, f32[32,128]{1,0:T(8,128)}, u32[]{:S(2)}) copy-start(f32[32,128]{1,0:T(8,128)} %constant.27.clone.ti_ref) | copy-start | bytes 49156
  0.7 16.8 %copy-start.7 = (f32[32,128]{1,0:T(8,128)S(1)}, f32[32,128]{1,0:T(8,128)}, u32[]{:S(2)}) copy-start(f32[32,128]{1,0:T(8,128)} %constant.26.clone.tr_ref) | copy-start | bytes 49156
